TPU v7x, 512 devices: a whole 4x8x8 slice. The times are simulated.
512 devices in a mesh: grp: 128 (over y, x_lo, z), blk: 4 (over x_hi, core).
Axes of the slice: x: 4 (x_hi: 2, x_lo: 2; x = x_hi * 2 + x_lo), y: 8, z: 8, core: 2. Of those that a mesh axis runs over, the one named last changes fastest.
Arguments:
- amplitudes: bfloat16 [2048, 128, 512], P('grp', 'blk'), may hold values from -6 to 6
- integrals: float32 [2048, 12, 128, 128], P(('grp', 'blk')), may hold values from -0.15625 to 0.15625
- tile_rows: int32 [2048, 12], P(('grp', 'blk')), may hold values from 0 to 2047, as said below
- destinations: int32 [2048, 4], replicated, may hold values from 0 to 127, as said below
- source_terms: bfloat16 [262144, 512], P(('grp', 'blk')), may hold values from -6 to 6
- occ_energy: float32 [512], replicated, may hold values from 0.5 to 4
- virt_energy: float32 [262144], P(('grp', 'blk')), may hold values from 0.5 to 4
Outputs:
- new_amplitudes: bfloat16 [262144, 512], P(('grp', 'blk'))
Inputs may be any that keep to these rules, and one draw needn't show every extreme that they name: `destinations`: each row names 4 different groups. Every group is named by exactly 64 rows in all. Among the 16 rows k of one owning group k // 16, no group is named by more than 2 rows, and that many is reached. `tile_rows`: the 12 entries of a row are different.
All inputs are finite; a program needn't handle non-finite values.
Results may differ from a plain program's by a relative error of at most 0.001.
Values may be sent and summed in bfloat16 or wider, within the bound.
No kernel may reach another device: no remote copies, remote signals or barrier semaphores. Data moves between devices by JAX's collectives and lax.ppermute only.
A program may use at most 64 MiB of HBM per device.

v0:
```python
import jax
import jax.numpy as jnp
from jax import lax
from jax.sharding import PartitionSpec as P

DEST = 4


def per_device(
    amplitudes, integrals, tile_rows, destinations, source_terms, occ_energy, virt_energy
):
    groups = lax.axis_size("grp")
    own_group = lax.axis_index("grp")
    owned_tiles = amplitudes.shape[0]
    quarter = amplitudes.shape[1]
    pair_width = amplitudes.shape[2]
    all_tiles = destinations.shape[0]
    slot_count = max(2, owned_tiles * DEST // groups)
    my_dest = lax.dynamic_slice_in_dim(destinations, own_group * owned_tiles, owned_tiles, 0)
    targets = jnp.arange(groups, dtype=jnp.int32)
    named_mine = jnp.any(my_dest[:, :, None] == targets[None, None, :], axis=1).astype(jnp.int32)
    before = jnp.cumsum(named_mine, axis=0) - named_mine
    slot_of = jnp.take_along_axis(before, my_dest, axis=1)
    send_place = my_dest * slot_count + slot_of
    select = jnp.any(
        jnp.arange(groups * slot_count, dtype=jnp.int32)[:, None, None] == send_place[None, :, :],
        axis=2,
    )
    select = select.astype(jnp.bfloat16)
    outgoing = jnp.dot(
        select,
        amplitudes.reshape(owned_tiles, quarter * pair_width),
        preferred_element_type=jnp.float32,
    )
    outgoing = outgoing.astype(jnp.bfloat16).reshape(groups * slot_count, quarter, pair_width)
    named_all = jnp.any(destinations == own_group, axis=1).astype(jnp.int32)
    per_source = named_all.reshape(groups, owned_tiles)
    slot_all = (jnp.cumsum(per_source, axis=1) - per_source).reshape(all_tiles)
    source_of = jnp.arange(all_tiles, dtype=jnp.int32) // owned_tiles
    position = source_of * slot_count + slot_all
    compact_of = jnp.cumsum(named_all) - named_all
    received = owned_tiles * DEST
    matches = (compact_of[None, :] == jnp.arange(received, dtype=jnp.int32)[:, None]) & (
        named_all[None, :] == 1
    )
    pick_rows = jnp.sum(jnp.where(matches, position[None, :], 0), axis=1)
    delivered = named_all[tile_rows]
    slots_used = jnp.where(delivered == 1, compact_of[tile_rows], 0)
    weights = integrals * delivered.astype(jnp.float32)[:, :, None, None]
    columns, row_tiles = tile_rows.shape
    tile_size = integrals.shape[3]
    flat_slots = slots_used.reshape(columns * row_tiles)
    incoming = lax.all_to_all(outgoing, "grp", split_axis=0, concat_axis=0, tiled=True)
    gathered_rows = jnp.take(incoming, pick_rows, axis=0)
    arrived = lax.all_gather(gathered_rows, "blk", axis=1, tiled=True)
    rows_here = arrived.shape[1]
    width_here = arrived.shape[2]
    picked = jnp.take(arrived, flat_slots, axis=0).reshape(
        columns, row_tiles, rows_here, width_here
    )
    picked = picked.astype(jnp.float32)
    ladder = jnp.einsum("crqk,crqp->ckp", weights, picked, precision=lax.Precision.HIGHEST)
    ladder = ladder.reshape(columns * tile_size, pair_width)
    denominator = virt_energy[:, None] + occ_energy[None, :]
    return ((source_terms.astype(jnp.float32) + ladder) / denominator).astype(jnp.bfloat16)


def solution(mesh):
    in_specs = (
        P("grp", "blk", None),
        P(("grp", "blk"), None, None, None),
        P(("grp", "blk"), None),
        P(),
        P(("grp", "blk"), None),
        P(),
        P(("grp", "blk")),
    )
    out_specs = P(("grp", "blk"), None)
    return jax.shard_map(
        per_device, mesh=mesh, in_specs=in_specs, out_specs=out_specs, check_vma=False
    )
```

profile of v0, /device:TPU:1, one launch (start us, length us, event | category | flops | bytes accessed | tf_op | source)
XLA Modules:
  0.0 397.3 jit_solution(89998441502436940)
XLA Ops:
  6.5 0.0 copy-start
  6.5 0.8 constant_dynamic-slice_fusion
  7.3 0.1 fusion.10
  7.4 0.1 copy.28
  7.6 0.1 copy.22
  7.7 0.1 copy.23
  7.8 0.1 reshape.189
  7.8 0.8 gather_fusion.4
  8.6 0.1 reshape.192
  8.7 0.1 copy.24
  8.8 0.1 fusion.9
  8.9 0.0 copy-done
  8.9 0.3 copy.29
  9.2 5.6 %convolution_convert_fusion = bf16[256,16384]{1,0:T(8,128)(2,1)} fusion(pred[256,16]{0,1:T(8,128)(4,1)S(1)} %fusion.9, bf16[16,16384]{1,0:T(8,128)(2,1)S(1)} %bitcast.35), kind=kOutput, calls=%fused_computation.5 | convolution fusion | flops 138412032 | bytes 8916992 | tf_op jit(solution)/shard_map/dot_general | solution.py:30
  14.8 10.4 %copy.30 = bf16[32,8,32,512]{3,2,1,0:T(8,128)(2,1)} copy(bf16[32,8,32,512]{3,1,2,0:T(8,128)(2,1)} %bitcast.33) | data formatting | bytes 16777216
  25.2 0.0 copy-start.2
  25.2 19.9 %all-to-all-start = ((bf16[256,32,512]{2,1,0:T(8,128)(2,1)}), bf16[256,32,512]{2,1,0:T(8,128)(2,1)}, u32[]{:S(2)}, u32[]{:S(2)}) async-start(bf16[256,32,512]{2,1,0:T(8,128)(2,1)} %bitcast.32), calls=%async_computation | async-start | bytes 16777216 | tf_op jit(solution)/shard_map/all_to_all | solution.py:53
  45.2 0.0 copy-start.3
  45.2 0.2 all-gather.2.cloned.1.call-start
  45.4 0.0 copy-done.2
  45.5 0.1 reshape.156
  45.5 0.1 copy.18
  45.6 0.1 reduce_window_sum.45
  45.6 0.1 copy.19
  45.8 0.1 reduce_window_sum.46
  45.8 0.3 reduce-window.9
  46.1 0.1 slice.19
  46.2 0.1 slice_reduce_fusion
  46.3 0.1 convert_subtract_fusion.1
  46.4 0.2 select_reduce_fusion
  46.7 220.9 %all-to-all-done = bf16[256,32,512]{2,1,0:T(8,128)(2,1)} async-done(((bf16[256,32,512]{2,1,0:T(8,128)(2,1)}), bf16[256,32,512]{2,1,0:T(8,128)(2,1)}, u32[]{:S(2)}, u32[]{:S(2)}) %all-to-all-start) | async-done | bytes 8388640 | tf_op jit(solution)/shard_map/all_to_all | solution.py:53
  267.6 4.1 %gather_fusion.2 = bf16[64,32,512]{2,1,0:T(8,128)(2,1)S(1)} fusion(bf16[256,32,512]{2,1,0:T(8,128)(2,1)} %all-to-all-done, s32[1024]{0:T(1024)S(1)} %pad_clamp_fusion.1), kind=kCustom, calls=%fused_computation.2 | custom fusion | bytes 4194560 | tf_op jit(solution)/shard_map/jit(_take)/gather | solution.py:54
  271.6 1.6 broadcast_select_fusion
  273.3 0.0 all-gather.2.cloned.1.call-update
  273.3 0.0 copy-done.3
  273.3 0.1 reshape.159
  273.4 0.8 gather_fusion.1
  274.2 0.8 gather_fusion
  275.0 0.1 reshape.206
  275.1 0.1 reshape.199
  275.2 0.0 copy-start.6
  275.2 100.1 %all-gather.2.cloned.1.call-done = bf16[64,128,512]{2,1,0:T(8,128)(2,1)} async-done(((bf16[64,32,512]{2,1,0:T(8,128)(2,1)}), bf16[64,128,512]{2,1,0:T(8,128)(2,1)}) %all-gather.2.cloned.1.call-update) | async-done | bytes 8388624 | tf_op jit(solution)/shard_map/all_gather | solution.py:55
  375.3 8.4 %gather_fusion.3 = bf16[48,128,512]{2,1,0:T(8,128)(2,1)} fusion(bf16[64,128,512]{2,1,0:T(8,128)(2,1)} %all-gather.2.cloned.1.call-done, s32[1024]{0:T(1024)S(1)} %pad_clamp_fusion), kind=kCustom, calls=%fused_computation.3 | custom fusion | bytes 12583104 | tf_op jit(solution)/shard_map/jit(_take)/gather | solution.py:58
  383.7 0.0 copy-start.1
  383.7 0.0 copy-start.4
  383.7 0.0 copy-start.5
  383.7 0.0 copy-done.6
  383.7 5.7 %fusion = f32[4,128,512,1]{2,1,3,0:T(8,128)S(1)} fusion(bf16[4,12,128,512]{3,2,1,0:T(8,128)(2,1)} %bitcast.34, pred[4,12]{1,0:T(4,128)(4,1)S(1)} %compare_and_fusion.1, f32[4,12,128,128]{3,2,1,0:T(8,128)S(1)} %copy-done.6, f32[4,12]{1,0:T(4,128)S(1)} %reshape.199), kind=kOutput, calls=%fused_computation.6 | convolution fusion | flops 4835770368 | bytes 10486000 | tf_op jit(solution)/shard_map/crqk,crqp->ckp/dot_general | solution.py:62
  389.4 0.0 copy-done.1
  389.4 0.0 copy-done.4
  389.4 0.0 copy-done.5
  389.4 1.0 fusion.7
  (18 shorter events, 0.2 us)
Async XLA Ops:
  6.5 2.4 copy-start
  25.2 20.2 %copy-start.2 = (s32[2048,4]{0,1:T(4,128)S(1)}, s32[2048,4]{0,1:T(4,128)}, u32[]{:S(2)}) copy-start(s32[2048,4]{0,1:T(4,128)} %param.10) | copy-start | bytes 98308
  25.2 242.4 %all-to-all-start = ((bf16[256,32,512]{2,1,0:T(8,128)(2,1)}), bf16[256,32,512]{2,1,0:T(8,128)(2,1)}, u32[]{:S(2)}, u32[]{:S(2)}) async-start(bf16[256,32,512]{2,1,0:T(8,128)(2,1)} %bitcast.32), calls=%async_computation | async-start | bytes 16777216 | tf_op jit(solution)/shard_map/all_to_all | solution.py:53
  45.2 228.2 %copy-start.3 = (s32[4,12]{1,0:T(4,128)S(1)}, s32[4,12]{1,0:T(4,128)}, u32[]{:S(2)}) copy-start(s32[4,12]{1,0:T(4,128)} %param.9) | copy-start | bytes 580
  45.2 330.1 %all-gather.2.cloned.1.call-start = ((), (), s32[]{:S(2)}) async-start(), calls=%async_computation.1 | async-start | bytes 10485760 | tf_op jit(solution)/shard_map/all_gather | solution.py:55
  275.2 108.5 %copy-start.6 = (f32[4,12,128,128]{3,2,1,0:T(8,128)S(1)}, f32[4,12,128,128]{3,2,1,0:T(8,128)}, u32[]{:S(2)}) copy-start(f32[4,12,128,128]{3,2,1,0:T(8,128)} %param.8) | copy-start | bytes 9437188
  383.7 5.7 %copy-start.1 = (bf16[512,512]{1,0:T(8,128)(2,1)S(1)}, bf16[512,512]{1,0:T(8,128)(2,1)}, u32[]{:S(2)}) copy-start(bf16[512,512]{1,0:T(8,128)(2,1)} %param.11) | copy-start | bytes 1572868
  383.7 5.7 %copy-start.4 = (f32[512]{0:T(512)S(1)}, f32[512]{0:T(512)}, u32[]{:S(2)}) copy-start(f32[512]{0:T(512)} %param.12) | copy-start | bytes 6148
  383.7 5.7 %copy-start.5 = (f32[512]{0:T(512)S(1)}, f32[512]{0:T(512)}, u32[]{:S(2)}) copy-start(f32[512]{0:T(512)} %param.13) | copy-start | bytes 6148
Sparse Core Ops, SparseCore 0:
  273.4 101.8 all-gather.1
where the time goes:
time: 398 us; the launch traced here: 397 us
  waiting for transfers between devices  321 us (81%)
  local copies, waits for them, and re-layouts  27.6 us (7%)
  starting transfers between devices  20.2 us (5%)
  between operations  13.6 us (3%)
  matrix products  11.3 us (3%)
    all_to_all x1, waiting for transfers between devices, per_device(): lax.all_to_all(outgoing, 'grp', split_axis=0, concat_axis=0, tiled=True)  221 us
    all_gather x1, waiting for transfers between devices, per_device(): arrived = lax.all_gather(gathered_rows, 'blk', axis=1, tiled=True)  100 us
    all_to_all x1, starting transfers between devices, per_device(): lax.all_to_all(outgoing, 'grp', split_axis=0, concat_axis=0, tiled=True)  19.9 us
    unnamed x17, local copies, waits for them, and re-layouts  10.8 us
    gather x1, local copies, waits for them, and re-layouts, per_device(): jnp.take(arrived, flat_slots, axis=0)  8.38 us
  transfers between devices with their start and end apart: 2, of which 2 were waited for; matrix products, arithmetic and copies ran while one was open for 1% of the time, Pallas kernels for 0%

commit v1 on v0

--- a/solution.py
+++ b/solution.py
@@ -4,6 +4,11 @@
 from jax.sharding import PartitionSpec as P
 
 DEST = 4
+
+
+def process_skins(u_in):
+    piece_now = jnp.stack(lax.axis_size("blk") * [u_in], axis=0)
+    return jnp.concatenate(lax.all_to_all(piece_now, "blk", 0, 0), axis=1)
 
 
 def per_device(
@@ -52,7 +57,7 @@
     flat_slots = slots_used.reshape(columns * row_tiles)
     incoming = lax.all_to_all(outgoing, "grp", split_axis=0, concat_axis=0, tiled=True)
     gathered_rows = jnp.take(incoming, pick_rows, axis=0)
-    arrived = lax.all_gather(gathered_rows, "blk", axis=1, tiled=True)
+    arrived = process_skins(gathered_rows)
     rows_here = arrived.shape[1]
     width_here = arrived.shape[2]
     picked = jnp.take(arrived, flat_slots, axis=0).reshape(

time: 398 us -> 431 us (1.083)
  the two profiles are of different devices: /device:TPU:1 before, /device:TPU:32 now
where the time goes in v1:
time: 431 us; the launch traced here: 430 us
  waiting for transfers between devices  352 us (82%)
  local copies, waits for them, and re-layouts  40.2 us (9%)
  starting transfers between devices  24.8 us (6%)
  matrix products  11.3 us (3%)
    all_to_all x1, waiting for transfers between devices, per_device(): lax.all_to_all(outgoing, 'grp', split_axis=0, concat_axis=0, tiled=True)  259 us
    all_to_all x1, waiting for transfers between devices, process_skins(): return jnp.concatenate(lax.all_to_all(piece_now, 'blk', 0, 0), axis=1)  92.6 us
    all_to_all x1, starting transfers between devices, per_device(): lax.all_to_all(outgoing, 'grp', split_axis=0, concat_axis=0, tiled=True)  18.9 us
    unnamed x17, local copies, waits for them, and re-layouts  10.8 us
  transfers between devices with their start and end apart: 2, of which 2 were waited for; matrix products, arithmetic and copies ran while one was open for 1% of the time, Pallas kernels for 0%

profile of v1, /device:TPU:32, one launch (start us, length us, event | category | flops | bytes accessed | tf_op | source)
XLA Modules:
  0.0 430.4 jit_solution(966563027569777628)
XLA Ops:
  0.0 0.0 copy-start
  0.0 0.8 constant_dynamic-slice_fusion
  0.8 0.1 fusion.10
  0.9 0.1 copy.36
  1.0 0.1 copy.29
  1.1 0.1 copy.30
  1.2 0.1 reshape.199
  1.3 0.8 gather_fusion.4
  2.1 0.1 reshape.202
  2.2 0.1 copy.31
  2.3 0.1 fusion.9
  2.4 0.0 copy-done
  2.4 0.3 copy.37
  2.7 5.6 %convolution_convert_fusion = bf16[256,16384]{1,0:T(8,128)(2,1)} fusion(pred[256,16]{0,1:T(8,128)(4,1)S(1)} %fusion.9, bf16[16,16384]{1,0:T(8,128)(2,1)S(1)} %bitcast.39), kind=kOutput, calls=%fused_computation.5 | convolution fusion | flops 138412032 | bytes 8916992 | tf_op jit(solution)/shard_map/dot_general | solution.py:35
  8.3 10.4 %copy.38 = bf16[32,8,32,512]{3,2,1,0:T(8,128)(2,1)} copy(bf16[32,8,32,512]{3,1,2,0:T(8,128)(2,1)} %bitcast.36) | data formatting | bytes 16777216
  18.7 0.0 copy-start.2
  18.7 18.9 %all-to-all-start = ((bf16[256,32,512]{2,1,0:T(8,128)(2,1)}), bf16[256,32,512]{2,1,0:T(8,128)(2,1)}, u32[]{:S(2)}, u32[]{:S(2)}) async-start(bf16[256,32,512]{2,1,0:T(8,128)(2,1)} %bitcast.35), calls=%async_computation | async-start | bytes 16777216 | tf_op jit(solution)/shard_map/all_to_all | solution.py:58
  37.5 0.0 copy-done.2
  37.6 0.3 reduce-window.9
  37.9 0.1 slice.19
  38.0 0.1 reshape.166
  38.1 0.1 copy.25
  38.1 0.1 reduce_window_sum.45
  38.2 0.1 copy.26
  38.3 0.1 reduce_window_sum.46
  38.4 0.1 slice_reduce_fusion
  38.5 0.1 convert_subtract_fusion.1
  38.6 0.2 select_reduce_fusion
  38.8 259.0 %all-to-all-done = bf16[256,32,512]{2,1,0:T(8,128)(2,1)} async-done(((bf16[256,32,512]{2,1,0:T(8,128)(2,1)}), bf16[256,32,512]{2,1,0:T(8,128)(2,1)}, u32[]{:S(2)}, u32[]{:S(2)}) %all-to-all-start) | async-done | bytes 8388640 | tf_op jit(solution)/shard_map/all_to_all | solution.py:58
  297.8 4.1 gather_fusion.2
  301.9 0.3 broadcast_select_fusion
  302.2 4.3 stack.2
  306.4 0.0 copy-start.3
  306.4 6.0 %all-to-all-start.1 = ((bf16[4,64,32,512]{3,2,1,0:T(8,128)(2,1)}), bf16[4,64,32,512]{3,2,1,0:T(8,128)(2,1)}, u32[]{:S(2)}, u32[]{:S(2)}) async-start(bf16[4,64,32,512]{3,2,1,0:T(8,128)(2,1)} %stack.2), calls=%async_computation.1 | async-start | bytes 16777216 | tf_op jit(solution)/shard_map/all_to_all | solution.py:11
  312.4 0.0 copy-done.3
  312.4 0.1 reshape.169
  312.5 0.8 gather_fusion
  313.3 0.8 gather_fusion.1
  314.1 0.1 reshape.209
  314.2 0.1 reshape.216
  314.3 92.6 %all-to-all-done.1 = bf16[4,64,32,512]{3,2,1,0:T(8,128)(2,1)} async-done(((bf16[4,64,32,512]{3,2,1,0:T(8,128)(2,1)}), bf16[4,64,32,512]{3,2,1,0:T(8,128)(2,1)}, u32[]{:S(2)}, u32[]{:S(2)}) %all-to-all-start.1) | async-done | bytes 8388640 | tf_op jit(solution)/shard_map/all_to_all | solution.py:11
  406.9 8.3 %copy.32 = bf16[4,64,32,512]{3,2,0,1:T(8,128)(2,1)} copy(bf16[4,64,32,512]{3,2,1,0:T(8,128)(2,1)} %all-to-all-done.1) | data formatting | bytes 16777216 | tf_op jit(solution)/shard_map/all_to_all | solution.py:11
  415.1 0.0 copy-start.6
  415.1 8.5 %gather_fusion.3 = bf16[48,128,512]{2,1,0:T(8,128)(2,1)} fusion(bf16[64,128,512]{2,1,0:T(8,128)(2,1)} %bitcast.37, s32[1024]{0:T(1024)S(1)} %pad_clamp_fusion), kind=kCustom, calls=%fused_computation.3 | custom fusion | bytes 12583104 | tf_op jit(solution)/shard_map/jit(_take)/gather | solution.py:63
  423.6 0.0 copy-start.1
  423.6 0.0 copy-start.4
  423.6 0.0 copy-start.5
  423.6 0.0 copy-done.6
  423.6 5.7 %fusion = f32[4,128,512,1]{2,1,3,0:T(8,128)S(1)} fusion(bf16[4,12,128,512]{3,2,1,0:T(8,128)(2,1)} %bitcast.38, pred[4,12]{1,0:T(4,128)(4,1)S(1)} %compare_and_fusion.1, f32[4,12,128,128]{3,2,1,0:T(8,128)S(1)} %copy-done.6, f32[4,12]{1,0:T(4,128)S(1)} %reshape.209), kind=kOutput, calls=%fused_computation.6 | convolution fusion | flops 4835770368 | bytes 10486000 | tf_op jit(solution)/shard_map/crqk,crqp->ckp/dot_general | solution.py:67
  429.3 0.0 copy-done.1
  429.4 0.0 copy-done.4
  429.4 0.0 copy-done.5
  429.4 1.0 fusion.7
  (18 shorter events, 0.2 us)
Async XLA Ops:
  0.0 2.4 copy-start
  18.7 18.9 %copy-start.2 = (s32[2048,4]{0,1:T(4,128)S(1)}, s32[2048,4]{0,1:T(4,128)}, u32[]{:S(2)}) copy-start(s32[2048,4]{0,1:T(4,128)} %param.10) | copy-start | bytes 98308
  18.7 279.1 %all-to-all-start = ((bf16[256,32,512]{2,1,0:T(8,128)(2,1)}), bf16[256,32,512]{2,1,0:T(8,128)(2,1)}, u32[]{:S(2)}, u32[]{:S(2)}) async-start(bf16[256,32,512]{2,1,0:T(8,128)(2,1)} %bitcast.35), calls=%async_computation | async-start | bytes 16777216 | tf_op jit(solution)/shard_map/all_to_all | solution.py:58
  306.4 6.0 %copy-start.3 = (s32[4,12]{1,0:T(4,128)S(1)}, s32[4,12]{1,0:T(4,128)}, u32[]{:S(2)}) copy-start(s32[4,12]{1,0:T(4,128)} %param.9) | copy-start | bytes 580
  306.4 100.4 %all-to-all-start.1 = ((bf16[4,64,32,512]{3,2,1,0:T(8,128)(2,1)}), bf16[4,64,32,512]{3,2,1,0:T(8,128)(2,1)}, u32[]{:S(2)}, u32[]{:S(2)}) async-start(bf16[4,64,32,512]{3,2,1,0:T(8,128)(2,1)} %stack.2), calls=%async_computation.1 | async-start | bytes 16777216 | tf_op jit(solution)/shard_map/all_to_all | solution.py:11
  415.1 8.5 %copy-start.6 = (f32[4,12,128,128]{3,2,1,0:T(8,128)S(1)}, f32[4,12,128,128]{3,2,1,0:T(8,128)}, u32[]{:S(2)}) copy-start(f32[4,12,128,128]{3,2,1,0:T(8,128)} %param.8) | copy-start | bytes 9437188
  423.6 5.7 %copy-start.1 = (bf16[512,512]{1,0:T(8,128)(2,1)S(1)}, bf16[512,512]{1,0:T(8,128)(2,1)}, u32[]{:S(2)}) copy-start(bf16[512,512]{1,0:T(8,128)(2,1)} %param.11) | copy-start | bytes 1572868
  423.6 5.7 %copy-start.4 = (f32[512]{0:T(512)S(1)}, f32[512]{0:T(512)}, u32[]{:S(2)}) copy-start(f32[512]{0:T(512)} %param.12) | copy-start | bytes 6148
  423.6 5.7 %copy-start.5 = (f32[512]{0:T(512)S(1)}, f32[512]{0:T(512)}, u32[]{:S(2)}) copy-start(f32[512]{0:T(512)} %param.13) | copy-start | bytes 6148
